TPU v7x, 256 devices: a whole 4x4x8 slice. The times are simulated.
256 devices in a mesh: parts: 256 (over x, y, z, core).
Axes of the slice: x: 4, y: 4, z: 8, core: 2. Of those that a mesh axis runs over, the one named last changes fastest.
Arguments:
- features: bfloat16 [524288, 256], P('parts'), may hold values from -32 to 32, as said below
- tile_values: bfloat16 [65536, 128, 128], P('parts'), may hold values from -0.0078125 to 0.009338379
- tile_blocks: int32 [65536, 2], P('parts'), may hold values from 0 to 23, as said below
- tile_count: int32 [256], P('parts'), may hold values from 24 to 256, as said below
- send_rows: int32 [256, 4, 256], P('parts'), may hold values from 0 to 2047, as said below
- recv_index: int32 [256, 1024], P('parts'), may hold values from 0 to 1023, as said below
- layer_weight: bfloat16 [2, 256, 256], replicated, may hold values from -0.375 to 0.375
- norm_gain: float32 [2, 256], replicated, may hold values from 0.1 to 1.9
- norm_shift: float32 [2, 256], replicated, may hold values from -3 to 3
Outputs:
- embedded: bfloat16 [524288, 256], P('parts')
Inputs may be any that keep to these rules, and one draw needn't show every extreme that they name: `features`: every entry is finite. `tile_blocks`: column 0 is a row block (0 to 15), column 1 a column block of columns_l. A device's first 16 tiles are the diagonal blocks (t, t) in order; the next 8 tiles have the column blocks 2048 // 128, 17, ... in order; blocks may repeat. `tile_count`: the live tiles are the leading ones of a device's list; some device has all 256 live in every draw. `send_rows`: entry [q, n] lists 256 distinct local rows that device q sends to device q + o[n], o = (1, -1, 2, -2). `recv_index`: each device's row is a permutation.
All inputs are finite; a program needn't handle non-finite values.
Results may differ from a plain program's by a relative error of at most 0.0072.
Values may be sent and summed in bfloat16 or wider, within the bound.
No kernel may reach another device: no remote copies, remote signals or barrier semaphores. Data moves between devices by JAX's collectives and lax.ppermute only.
A program may use at most 64 MiB of HBM per device.

v0:
```python
import functools

import jax
import jax.numpy as jnp
from jax import lax
from jax.experimental import pallas as pl
from jax.experimental.pallas import tpu as pltpu
from jax.sharding import Mesh
from jax.sharding import PartitionSpec as P


PARTS = ("parts_0", "parts_1", "parts_2", "parts_3")
PLANE = PARTS[:2]
COLUMN = PARTS[2:]
norm_eps = 1e-05
EDGE = 128
MIB = 1 << 20


def swap(value, first, stride, total):
    pairs = []
    for q in range(total - stride):
        if first(q):
            pairs += [(q, q + stride), (q + stride, q)]
    return lax.ppermute(value, PARTS, pairs)


def chip_swaps(to_c, to_d):
    total = lax.axis_size(PARTS)
    got_d = swap(to_d, lambda q: q % 4 >= 2, 2, total)
    got_c = swap(to_c, lambda q: q % 4 < 2, 2, total)
    return got_c, got_d


def core_swap(value):
    return swap(value, lambda q: q % 2 == 0, 1, lax.axis_size(PARTS))


def fill_one_hot(index_ref, one_hot_ref, groups):
    columns = one_hot_ref.shape[1]
    lanes = lax.broadcasted_iota(jnp.int32, (EDGE, EDGE), 1)
    for group in groups:
        row = jnp.broadcast_to(index_ref[pl.ds(group, 1), :], (EDGE, EDGE))
        away = row.T - lanes
        for block in range(columns // EDGE):
            one_hot_ref[pl.ds(group * EDGE, EDGE), pl.ds(block * EDGE, EDGE)] = jnp.where(
                away == block * EDGE, 1.0, 0.0
            ).astype(jnp.bfloat16)


def pick_piece(one_hot_ref, rows_ref, piece_ref, first, at, count):
    piece_ref[pl.ds(at, count), :] = jnp.dot(
        one_hot_ref[pl.ds(first, count), :], rows_ref[...], preferred_element_type=jnp.float32
    ).astype(jnp.bfloat16)


def pick_payloads(one_hot_ref, rows_ref, to_c, to_d):
    size = to_c.shape[0]
    pick_piece(one_hot_ref, rows_ref, to_c, 0, 0, size)
    pick_piece(one_hot_ref, rows_ref, to_d, size, 0, size)


def spread(row):
    n = row.shape[1]
    return jnp.broadcast_to(row, (n, n)).T


def put_tile_order(blocks_ref, live_count, row_count, column_count, order_ref):
    tiles = blocks_ref.shape[1]
    number = lax.broadcasted_iota(jnp.int32, (1, tiles), 1)
    live = number < live_count
    row = jnp.where(live, blocks_ref[0:1, :], 0)
    column = jnp.where(live, blocks_ref[1:2, :], column_count)
    cell = column * row_count + row
    key = cell * tiles + number
    down = lax.broadcasted_iota(jnp.int32, (tiles, tiles), 0)
    cells_down = spread(cell)
    keys_down = cells_down * tiles + down
    rank = jnp.sum((keys_down < key).astype(jnp.int32), axis=0, keepdims=True)
    same = (cells_down == cell) & (down < number)
    keep = jnp.sum(same.astype(jnp.int32), axis=0, keepdims=True) > 0
    packed = (cell * 2 + keep.astype(jnp.int32)) * tiles + number
    hit = spread(rank) == number
    packed = jnp.sum(jnp.where(hit, spread(packed), 0), axis=0, keepdims=True)
    cell = packed // (2 * tiles)
    order_ref[0:1, :] = packed % tiles
    order_ref[1:2, :] = cell % row_count
    order_ref[2:3, :] = cell // row_count
    order_ref[3:4, :] = (packed // tiles) % 2


def put_zeros(dense_ref, first, last):
    size = 256
    zeros = jnp.zeros((size, dense_ref.shape[2]), dense_ref.dtype)

    @pl.loop(first, last)
    def _(c):
        for at in range(0, dense_ref.shape[1], size):
            dense_ref[c, pl.ds(at, size), :] = zeros


def gather_kernel(row_count, column_count, zeroed, loaded,
                  device_ref, live_ref, send_in, blocks_in, features_ref, tiles_in,
                  to_c, to_d, near_ref, one_hot_ref, order_ref, rows_ref, dense_ref, tiles_ref,
                  send_ref, blocks_ref, index_ref, arrived):
    load_send = pltpu.make_async_copy(send_in, send_ref, arrived.at[0])
    load_blocks = pltpu.make_async_copy(blocks_in, blocks_ref, arrived.at[1])
    load = pltpu.make_async_copy(features_ref, rows_ref, arrived.at[2])
    part = pl.ds(0, loaded)
    load_tiles = pltpu.make_async_copy(tiles_in.at[part], tiles_ref.at[part], arrived.at[3])
    load_send.start()
    load_blocks.start()
    load.start()
    load_tiles.start()
    put_zeros(dense_ref, 0, zeroed)
    load_send.wait()
    even_chip = device_ref[0] % 4 < 2
    count = send_ref.shape[1]
    per_piece = count // EDGE
    for part in range(per_piece):
        n0, n1, n2, n3 = (send_ref[n:n + 1, part * EDGE:(part + 1) * EDGE] for n in range(4))
        lists = (
            jnp.where(even_chip, n2, n3),
            jnp.where(even_chip, n0, n1),
            jnp.where(even_chip, n3, n2),
            jnp.where(even_chip, n1, n0),
        )
        for n, chosen in enumerate(lists):
            at = n * per_piece + part
            index_ref[at:at + 1, :] = chosen
    fill_one_hot(index_ref, one_hot_ref, range(2 * per_piece))
    load_blocks.wait()
    put_tile_order(blocks_ref, live_ref[0], row_count, column_count, order_ref)
    load.wait()
    pick_piece(one_hot_ref, rows_ref, to_c, 0, 0, count)
    fill_one_hot(index_ref, one_hot_ref, range(2 * per_piece, 3 * per_piece))
    pick_piece(one_hot_ref, rows_ref, to_c, count, count, count)
    fill_one_hot(index_ref, one_hot_ref, range(3 * per_piece, 4 * per_piece))
    pick_piece(one_hot_ref, rows_ref, to_d, 2 * count, 0, count)
    pick_piece(one_hot_ref, rows_ref, to_d, 3 * count, count, count)
    put_near(device_ref, to_c, to_d, near_ref, 0)
    load_tiles.wait()


def put_near(device_ref, from_c, from_d, out_ref, at):
    count = from_c.shape[0] // 2
    first = (device_ref[0] % 4 < 2) == (device_ref[0] % 2 == 0)

    @pl.when(first)
    def _():
        out_ref[at:at + count, :] = from_c[count:2 * count, :]

    @pl.when(jnp.logical_not(first))
    def _():
        out_ref[at:at + count, :] = from_d[count:2 * count, :]


def relay_kernel(after_ref, device_ref, near_ref, got_c, got_d, out_ref):
    del after_ref
    count = near_ref.shape[0]
    out_ref[0:count, :] = near_ref[...]
    put_near(device_ref, got_c, got_d, out_ref, count)


def put_total(parts_ref, out_ref):
    both = jnp.sum(parts_ref[...], axis=0)
    for n in range(out_ref.shape[0]):
        out_ref[n] = both


def adjacency_block(dense_ref, first, last, start, size):
    return jnp.concatenate(
        [dense_ref[c, pl.ds(start, size), :] for c in range(first, last)], axis=1
    )


def build_kernel(count, zeroed, loaded,
                 device_ref, order_ref, live_ref, recv_in, tiles_in, _dense, _tiles,
                 dense_ref, held_ref, recv_hot_ref, index_ref, recv_ref, arrived):
    part = pl.ds(loaded, held_ref.shape[0] - loaded)
    load_recv = pltpu.make_async_copy(recv_in, recv_ref, arrived.at[0])
    load = pltpu.make_async_copy(tiles_in.at[part], held_ref.at[part], arrived.at[1])
    load_recv.start()
    load.start()
    unroll = 8
    put_zeros(dense_ref, zeroed, dense_ref.shape[0])

    near = jnp.where(device_ref[0] % 2 == 0, count, 0)
    far = jnp.where(device_ref[0] % 4 < 2, count, 0)
    load_recv.wait()
    for group in range(index_ref.shape[0]):
        rows = recv_ref[0:1, group * EDGE:(group + 1) * EDGE]
        index_ref[group:group + 1, :] = rows ^ jnp.where(rows < 2 * count, near, far)
    fill_one_hot(index_ref, recv_hot_ref, range(index_ref.shape[0]))
    load.wait()

    def step(turn, total):
        for u in range(unroll):
            k = turn * unroll + u
            tile = held_ref[order_ref[0, k]].astype(jnp.float32)
            total = total * order_ref[3, k].astype(jnp.float32) + tile
            start = pl.multiple_of(order_ref[1, k] * EDGE, EDGE)
            dense_ref[order_ref[2, k], pl.ds(start, EDGE), :] = total.astype(jnp.bfloat16)
        return total

    lax.fori_loop(
        0, (live_ref[0] + unroll - 1) // unroll, step, jnp.zeros((EDGE, EDGE), jnp.float32)
    )


def own_kernel(dense_ref, rows_ref, own_ref, dense_out, left):
    store = pltpu.make_async_copy(
        dense_ref.at[pl.ds(0, dense_out.shape[0])], dense_out, left
    )
    store.start()
    height = own_ref.shape[0]
    own_blocks = height // EDGE
    size = 512
    for start in range(0, height, size):
        own_ref[pl.ds(start, size), :] = jnp.dot(
            adjacency_block(dense_ref, 0, own_blocks, start, size),
            rows_ref[...],
            preferred_element_type=jnp.float32,
        )
    store.wait()


def add_moments(z, moment_ref):
    wide = z.astype(jnp.float32)
    moment_ref[0:8, :] += jnp.sum(wide.reshape(-1, 8, wide.shape[1]), axis=0)
    moment_ref[8:16, :] += jnp.sum(jnp.square(wide).reshape(-1, 8, wide.shape[1]), axis=0)


def put_moments(moment_ref, out_ref):
    both = jnp.concatenate(
        [
            jnp.sum(moment_ref[0:8, :], axis=0, keepdims=True),
            jnp.sum(moment_ref[8:16, :], axis=0, keepdims=True),
        ],
        axis=0,
    )
    for n in range(out_ref.shape[0]):
        out_ref[n] = both


def received(a, c, d):
    count = a.shape[0] // 2
    return a[0:count, :], a[count:2 * count, :], c[0:count, :], d[0:count, :]


def first_kernel(device_ref, recv_hot_ref, a, c, d, dense_ref, own_ref, weight_ref, send_hot_ref,
                 z_ref, stats_ref, to_c, to_d, near_ref, dense_out,
                 halo_ref, got_ref, moment_ref, left):
    layer = 0
    count = a.shape[0] // 2
    written = own_ref.shape[0] // EDGE + 4 * count // EDGE - dense_out.shape[0]
    store = pltpu.make_async_copy(
        dense_ref.at[pl.ds(written, dense_out.shape[0])], dense_out, left
    )
    store.start()
    for n, piece in enumerate(received(a, c, d)):
        got_ref[pl.ds(n * count, count), :] = piece
    halo_ref[...] = jnp.dot(
        recv_hot_ref[...], got_ref[...], preferred_element_type=jnp.float32
    ).astype(jnp.bfloat16)
    moment_ref[...] = jnp.zeros_like(moment_ref)
    height = z_ref.shape[0]
    own_blocks, halo_blocks = height // EDGE, halo_ref.shape[0] // EDGE
    size = 512

    @pl.loop(0, height // size)
    def _(m):
        start = pl.multiple_of(m * size, size)
        agg = own_ref[pl.ds(start, size), :] + jnp.dot(
            adjacency_block(dense_ref, own_blocks, own_blocks + halo_blocks, start, size),
            halo_ref[...],
            preferred_element_type=jnp.float32,
        )
        z = jnp.dot(
            agg.astype(jnp.bfloat16), weight_ref[layer], preferred_element_type=jnp.float32
        ).astype(jnp.bfloat16)
        z_ref[pl.ds(start, size), :] = z
        add_moments(z, moment_ref)

    put_moments(moment_ref, stats_ref)
    pick_payloads(send_hot_ref, z_ref, to_c, to_d)
    put_near(device_ref, to_c, to_d, near_ref, 0)
    store.wait()


def scale_of(stats_ref, gain_ref, shift_ref, layer, vertex_total):
    both = jnp.sum(stats_ref[...], axis=0) / vertex_total
    centre = both[0:1, :]
    spread = both[1:2, :] - jnp.square(centre)
    factor = gain_ref[layer:layer + 1, :] / jnp.sqrt(spread + norm_eps)
    return centre, factor, shift_ref[layer:layer + 1, :]


def normal(rows, terms):
    centre, factor, shift = terms
    return jnp.maximum((rows.astype(jnp.float32) - centre) * factor + shift, 0.0)


def second_kernel(device_total, device_ref, index_ref, a, c, d, mixed_ref, stats_in_ref,
                  gain_ref, shift_ref, dense_a, dense_b, weight_ref, z_ref, stats_ref,
                  got_ref, columns_ref, moment_ref, recv_hot_ref, dense_ref, arrived):
    layer = 1
    count = a.shape[0] // 2
    height = z_ref.shape[0]
    halo = 4 * count
    blocks = (height + halo) // EDGE
    size = dense_ref.shape[2]


    def loads(m):
        rows, at, found = pl.ds(pl.multiple_of(m * size, size), size), 0, []
        for n, part in enumerate((dense_a, dense_b)):
            found.append(pltpu.make_async_copy(
                part.at[:, rows, :], dense_ref.at[m, pl.ds(at, part.shape[0])], arrived.at[m, n]
            ))
            at += part.shape[0]
        return found

    for m in range(height // size):
        for load in loads(m):
            load.start()
    terms = scale_of(stats_in_ref, gain_ref, shift_ref, 0, device_total * height)
    device = device_ref[0]
    near_side = (device > 0) & (device < device_total - 1)
    far_side = (device > 1) & (device < device_total - 2)
    present = (1.0, near_side.astype(jnp.float32), 1.0, far_side.astype(jnp.float32))
    for n, piece in enumerate(received(a, c, d)):
        got_ref[pl.ds(n * count, count), :] = (
            normal(piece, terms) * present[n]
        ).astype(jnp.bfloat16)
    for part in range(8):
        rows = pl.ds(part * (height // 8), height // 8)
        columns_ref[rows, :] = normal(mixed_ref[rows, :], terms).astype(jnp.bfloat16)
    fill_one_hot(index_ref, recv_hot_ref, range(index_ref.shape[0]))
    columns_ref[pl.ds(height, halo), :] = jnp.dot(
        recv_hot_ref[...], got_ref[...], preferred_element_type=jnp.float32
    ).astype(jnp.bfloat16)
    moment_ref[...] = jnp.zeros_like(moment_ref)

    @pl.loop(0, height // size)
    def _(m):
        for load in loads(m):
            load.wait()
        start = pl.multiple_of(m * size, size)
        agg = jnp.dot(
            jnp.concatenate([dense_ref[m, c] for c in range(blocks)], axis=1),
            columns_ref[...],
            preferred_element_type=jnp.float32,
        )
        z = jnp.dot(
            agg.astype(jnp.bfloat16), weight_ref[layer], preferred_element_type=jnp.float32
        ).astype(jnp.bfloat16)
        z_ref[pl.ds(start, size), :] = z
        add_moments(z, moment_ref)

    put_moments(moment_ref, stats_ref)


def last_kernel(vertex_total, mixed_ref, stats_in_ref, gain_ref, shift_ref, out_ref):
    terms = scale_of(stats_in_ref, gain_ref, shift_ref, 1, vertex_total)
    out_ref[...] = normal(mixed_ref[...], terms).astype(jnp.bfloat16)


VMEM = pl.BlockSpec(memory_space=pltpu.VMEM)
SMEM = pl.BlockSpec(memory_space=pltpu.SMEM)
HBM = pl.BlockSpec(memory_space=pltpu.HBM)


def from_peers(stats, axes):
    return lax.all_to_all(stats, axes, 0, 0, tiled=True)


def shards(features, tile_values, tile_blocks, tile_count, send_rows, recv_index,
           layer_weight, norm_gain, norm_shift):
    height, channels = features.shape
    neighbours, count = send_rows.shape[1:]
    halo = neighbours * count
    row_count = height // EDGE
    column_count = (height + halo) // EDGE
    device = lax.axis_index(PARTS)
    total = lax.axis_size(PARTS)
    vertex_total = height * total
    peers = lax.axis_size(PLANE)
    bf16, f32 = jnp.bfloat16, jnp.float32
    struct = jax.ShapeDtypeStruct
    piece = struct((count, channels), bf16)
    payload = struct((2 * count, channels), bf16)
    stats_type = struct((peers, 2, channels), f32)
    mixed = struct((height, channels), bf16)

    place = device.reshape(1)

    def on_chip(value):
        return pltpu.with_memory_space_constraint(value, pltpu.VMEM)

    def in_hbm(value):
        return pltpu.with_memory_space_constraint(value, pltpu.HBM)

    zeroed, loaded = column_count // 2, tile_values.shape[0] * 5 // 8
    dense_type = pltpu.VMEM((column_count + 1, height, EDGE), bf16)
    tiles_type = pltpu.VMEM(tile_values.shape, bf16)
    *sent, near, send_hot, order, rows, dense, tiles = pl.pallas_call(
        functools.partial(gather_kernel, row_count, column_count, zeroed, loaded),
        out_shape=[payload] * 2 + [
            piece,
            pltpu.VMEM((halo, height), bf16),
            struct((4, tile_blocks.shape[0]), jnp.int32),
            pltpu.VMEM((height, channels), bf16),
            dense_type,
            tiles_type,
        ],
        in_specs=[SMEM, SMEM, HBM, HBM, HBM, HBM],
        out_specs=[VMEM] * 8,
        scratch_shapes=[
            pltpu.VMEM((neighbours, count), jnp.int32),
            pltpu.VMEM((2, tile_blocks.shape[0]), jnp.int32),
            pltpu.VMEM((halo // EDGE, EDGE), jnp.int32),
            pltpu.SemaphoreType.DMA((4,)),
        ],
        compiler_params=pltpu.CompilerParams(vmem_limit_bytes=16 * MIB),
        cost_estimate=pl.CostEstimate(
            flops=2 * halo * height * channels, bytes_accessed=2 * MIB, transcendentals=0),
    )(place, tile_count, in_hbm(send_rows[0]), in_hbm(tile_blocks.T), in_hbm(features),
      in_hbm(tile_values))
    got = chip_swaps(*sent)

    dense, _, recv_hot, built = pl.pallas_call(
        functools.partial(build_kernel, count, zeroed, loaded),
        out_shape=[
            dense_type,
            tiles_type,
            pltpu.VMEM((halo, halo), bf16),
            struct((halo // EDGE, EDGE), jnp.int32),
        ],
        in_specs=[SMEM, SMEM, SMEM, HBM, HBM, VMEM, VMEM],
        out_specs=[VMEM] * 4,
        input_output_aliases={5: 0, 6: 1},
        scratch_shapes=[
            pltpu.VMEM(recv_index.shape, jnp.int32),
            pltpu.SemaphoreType.DMA((2,)),
        ],
        compiler_params=pltpu.CompilerParams(vmem_limit_bytes=8 * MIB),
        cost_estimate=pl.CostEstimate(
            flops=4 * height * height * channels, bytes_accessed=24 * MIB, transcendentals=0),
    )(place, order, tile_count, in_hbm(recv_index), in_hbm(tile_values), on_chip(dense),
      on_chip(tiles))

    early = column_count // 3
    own, dense_a = pl.pallas_call(
        own_kernel,
        out_shape=[
            pltpu.VMEM((height, channels), f32),
            pltpu.HBM((early, height, EDGE), bf16),
        ],
        in_specs=[VMEM] * 2,
        out_specs=[VMEM, HBM],
        scratch_shapes=[pltpu.SemaphoreType.DMA],
        compiler_params=pltpu.CompilerParams(vmem_limit_bytes=8 * MIB),
        cost_estimate=pl.CostEstimate(
            flops=2 * height * height * channels, bytes_accessed=8 * MIB, transcendentals=0),
    )(on_chip(dense), on_chip(rows))

    relay_call = pl.pallas_call(
        relay_kernel,
        out_shape=payload,
        in_specs=[VMEM, SMEM] + [VMEM] * 3,
        out_specs=VMEM,
        compiler_params=pltpu.CompilerParams(vmem_limit_bytes=4 * MIB),
    )
    relay = relay_call(own, place, near, *got)
    got_core = core_swap(relay)

    z, stats, *sent, near, dense_b = pl.pallas_call(
        first_kernel,
        out_shape=[pltpu.VMEM(mixed.shape, bf16), pltpu.VMEM(stats_type.shape, f32)]
        + [payload] * 2 + [piece, pltpu.HBM((column_count - early, height, EDGE), bf16)],
        in_specs=[SMEM] + [VMEM] * 8,
        out_specs=[VMEM] * 5 + [HBM],
        scratch_shapes=[
            pltpu.VMEM((halo, channels), bf16),
            pltpu.VMEM((halo, channels), bf16),
            pltpu.VMEM((16, channels), f32),
            pltpu.SemaphoreType.DMA,
        ],
        compiler_params=pltpu.CompilerParams(vmem_limit_bytes=12 * MIB),
        cost_estimate=pl.CostEstimate(
            flops=2 * height * halo * channels, bytes_accessed=16 * MIB, transcendentals=0),
    )(place, on_chip(recv_hot), got_core, *got, on_chip(dense), on_chip(own), layer_weight, on_chip(send_hot))
    got = chip_swaps(*sent)
    stats = from_peers(stats, PLANE)
    column_stats = struct((lax.axis_size(COLUMN), 2, channels), f32)
    total_call = pl.pallas_call(
        put_total,
        out_shape=pltpu.VMEM(column_stats.shape, f32),
        in_specs=[VMEM],
        out_specs=VMEM,
        compiler_params=pltpu.CompilerParams(vmem_limit_bytes=MIB),
    )
    stats = from_peers(total_call(stats), COLUMN)
    relay = relay_call(built, place, near, *got)
    got_core = core_swap(relay)

    chunk = 512
    z, stats = pl.pallas_call(
        functools.partial(second_kernel, total),
        out_shape=[pltpu.VMEM(mixed.shape, bf16), stats_type],
        in_specs=[SMEM] + [VMEM] * 8 + [HBM, HBM, VMEM],
        out_specs=[VMEM] * 2,
        scratch_shapes=[
            pltpu.VMEM((halo, channels), bf16),
            pltpu.VMEM((height + halo, channels), bf16),
            pltpu.VMEM((16, channels), f32),
            pltpu.VMEM((halo, halo), bf16),
            pltpu.VMEM((height // chunk, column_count, chunk, EDGE), bf16),
            pltpu.SemaphoreType.DMA((height // chunk, 2)),
        ],
        compiler_params=pltpu.CompilerParams(vmem_limit_bytes=28 * MIB),
        cost_estimate=pl.CostEstimate(
            flops=2 * height * (height + halo) * channels, bytes_accessed=16 * MIB,
            transcendentals=0),
    )(place, built, got_core, *got, on_chip(z), stats, norm_gain, norm_shift,
      in_hbm(dense_a), in_hbm(dense_b), layer_weight)
    stats = from_peers(stats, PLANE)
    stats = from_peers(total_call(stats), COLUMN)

    return pl.pallas_call(
        functools.partial(last_kernel, vertex_total),
        out_shape=mixed,
        in_specs=[VMEM] * 4,
        out_specs=VMEM,
        compiler_params=pltpu.CompilerParams(vmem_limit_bytes=16 * MIB),
    )(on_chip(z), stats, norm_gain, norm_shift)


def solution(mesh):
    finer = Mesh(mesh.devices.reshape(4, 4, 8, 2), PARTS)
    placed = (
        P(PARTS, None),
        P(PARTS, None, None),
        P(PARTS, None),
        P(PARTS),
        P(PARTS, None, None),
        P(PARTS, None),
        P(),
        P(),
        P(),
    )
    return jax.shard_map(
        shards, mesh=finer, in_specs=placed, out_specs=P(PARTS, None), check_vma=False
    )
```

profile of v0, /device:TPU:1, one launch (start us, length us, event | category | flops | bytes accessed | tf_op | source)
XLA Modules:
  0.0 99.0 jit_solution(12958029000468670920)
XLA Ops:
  0.7 3.1 %shard_map.91 = (bf16[512,256]{1,0:T(8,128)(2,1)S(1)}, bf16[512,256]{1,0:T(8,128)(2,1)S(1)}, bf16[256,256]{1,0:T(8,128)(2,1)S(1)}, bf16[1024,2048]{1,0:T(8,128)(...) custom-call(s32[1]{0:T(128)} %bitcast.device_ref, ...), custom_call_target="tpu_custom_call" | custom-call | flops 1073741824 | bytes 2097152 | tf_op jit(solution)/shard_map/pallas_call | solution.py:407
  3.8 2.5 %collective-permute-start = (bf16[512,256]{1,0:T(8,128)(2,1)S(1)}, bf16[512,256]{1,0:T(8,128)(2,1)S(1)}, u32[]{:S(2)}, u32[]{:S(2)}) collective-permute-start(bf16[512,256]{1,0:T(8,128)(2,1)S(1)} %get-tuple-element.35), channel_id=1, source_target_pairs={{0,2},{2,0},{1,3},{3,1},{4,6},{6,4},{5,7},{7,5},{8,10},{10,8},{9,1... | collective-permute-start | bytes 786440 | tf_op jit(solution)/shard_map/ppermute | solution.py:25
  6.3 0.7 collective-permute-start.1
  7.0 2.8 %shard_map.92 = (bf16[25,2048,128]{2,1,0:T(8,128)(2,1)S(1)}, bf16[256,128,128]{2,1,0:T(8,128)(2,1)S(1)}, bf16[1024,1024]{1,0:T(8,128)(2,1)S(1)}, s32[8,128]{1,0:T(8,128)S(1)}) custom-call(s32[1]{0:T(128)} %bitcast.device_ref, s32[4,256]{1,0:T(4,128)S(1)} %get-tuple-element.26.order_ref, ...), custom_call_target="tpu_custom_call", output_to_operand_aliasing={{0}: (5, {}), {1}: (6, {})} | custom-call | flops 4294967296 | bytes 25165824 | tf_op jit(solution)/shard_map/pallas_call | solution.py:432
  9.8 0.0 copy-start
  9.8 2.3 %shard_map.93 = (f32[2048,256]{1,0:T(8,128)S(1)}, bf16[8,2048,128]{2,1,0:T(8,128)(2,1)}) custom-call(bf16[25,2048,128]{2,1,0:T(8,128)(2,1)S(1)} %get-tuple-element.31.dense_ref, bf16[2048,256]{1,0:T(8,128)(2,1)S(1)} %get-tuple-element.32.rows_ref), custom_call_target="tpu_custom_call" | custom-call | flops 2147483648 | bytes 8388608 | tf_op jit(solution)/shard_map/pallas_call | solution.py:454
  12.2 0.0 collective-permute-done.got_c.c
  12.2 0.0 collective-permute-done.1.got_d.d
  12.2 1.8 %collective-permute-start.2 = (bf16[512,256]{1,0:T(8,128)(2,1)S(1)}, bf16[512,256]{1,0:T(8,128)(2,1)S(1)}, u32[]{:S(2)}, u32[]{:S(2)}) collective-permute-start(bf16[512,256]{1,0:T(8,128)(2,1)S(1)} %shard_map.94), channel_id=1, source_target_pairs={{0,1},{1,0},{2,3},{3,2},{4,5},{5,4},{6,7},{7,6},{8,9},{9,8},{10,11... | collective-permute-start | bytes 786440 | tf_op jit(solution)/shard_map/ppermute | solution.py:25
  14.0 1.2 %collective-permute-done.2.a = bf16[512,256]{1,0:T(8,128)(2,1)S(1)} collective-permute-done((bf16[512,256]{1,0:T(8,128)(2,1)S(1)}, bf16[512,256]{1,0:T(8,128)(2,1)S(1)}, u32[]{:S(2)}, u32[]{:S(2)}) %collective-permute-start.2) | collective-permute-done | bytes 262176 | tf_op jit(solution)/shard_map/ppermute | solution.py:25
  15.2 0.0 copy-done
  15.2 0.0 copy-start.1
  15.2 0.0 copy-start.2
  15.2 4.6 %shard_map.95 = (bf16[2048,256]{1,0:T(8,128)(2,1)S(1)}, f32[16,2,256]{2,1,0:T(2,128)S(1)}, bf16[512,256]{1,0:T(8,128)(2,1)S(1)}, bf16[512,256]{1,0:T(8,128)(2,1)...) custom-call(s32[1]{0:T(128)} %bitcast.device_ref, ...), custom_call_target="tpu_custom_call" | custom-call | flops 1073741824 | bytes 16777216 | tf_op jit(solution)/shard_map/pallas_call | solution.py:478
  19.8 4.9 %collective-permute-start.3 = (bf16[512,256]{1,0:T(8,128)(2,1)S(1)}, bf16[512,256]{1,0:T(8,128)(2,1)S(1)}, u32[]{:S(2)}, u32[]{:S(2)}) collective-permute-start(bf16[512,256]{1,0:T(8,128)(2,1)S(1)} %get-tuple-element.39), channel_id=1, source_target_pairs={{0,2},{2,0},{1,3},{3,1},{4,6},{6,4},{5,7},{7,5},{8,10},{10,8},{9,1... | collective-permute-start | bytes 786440 | tf_op jit(solution)/shard_map/ppermute | solution.py:25
  24.7 0.7 collective-permute-start.4
  25.4 5.6 %collective-permute-done.3.got_c.c = bf16[512,256]{1,0:T(8,128)(2,1)S(1)} collective-permute-done((bf16[512,256]{1,0:T(8,128)(2,1)S(1)}, bf16[512,256]{1,0:T(8,128)(2,1)S(1)}, u32[]{:S(2)}, u32[]{:S(2)}) %collective-permute-start.3) | collective-permute-done | bytes 262176 | tf_op jit(solution)/shard_map/ppermute | solution.py:25
  31.0 0.0 collective-permute-done.4.got_d.d
  31.1 1.0 %collective-permute-start.5 = (bf16[512,256]{1,0:T(8,128)(2,1)S(1)}, bf16[512,256]{1,0:T(8,128)(2,1)S(1)}, u32[]{:S(2)}, u32[]{:S(2)}) collective-permute-start(bf16[512,256]{1,0:T(8,128)(2,1)S(1)} %shard_map.96), channel_id=1, source_target_pairs={{0,1},{1,0},{2,3},{3,2},{4,5},{5,4},{6,7},{7,6},{8,9},{9,8},{10,11... | collective-permute-start | bytes 786440 | tf_op jit(solution)/shard_map/ppermute | solution.py:25
  32.1 22.6 %all_to_all.20.parts_ref = f32[16,2,256]{2,1,0:T(2,128)S(1)} all-to-all(f32[16,2,256]{2,1,0:T(2,128)S(1)} %get-tuple-element.42), channel_id=1, replica_groups=mesh['parts_0'=4,'parts_1'=4,'parts_2'=8,'parts_3'=2] {'parts_0','parts_1'}, dimensions={0} | all-to-all | bytes 65536 | tf_op jit(solution)/shard_map/all_to_all | solution.py:375
  54.8 15.1 %all_to_all.21.stats_in_ref = f32[16,2,256]{2,1,0:T(2,128)S(1)} all-to-all(f32[16,2,256]{2,1,0:T(2,128)S(1)} %shard_map.97), channel_id=1, replica_groups=mesh['parts_0'=4,'parts_1'=4,'parts_2'=8,'parts_3'=2] {'parts_2','parts_3'}, dimensions={0} | all-to-all | bytes 65536 | tf_op jit(solution)/shard_map/all_to_all | solution.py:375
  69.8 0.0 collective-permute-done.5.a
  69.9 0.0 copy-done.1
  69.9 0.0 copy-done.2
  69.9 6.8 %shard_map.98 = (bf16[2048,256]{1,0:T(8,128)(2,1)S(1)}, f32[16,2,256]{2,1,0:T(2,128)S(1)}) custom-call(s32[1]{0:T(128)} %bitcast.device_ref, s32[8,128]{1,0:T(8,128)S(1)} %get-tuple-element.29.after_ref.index_ref, bf16[512,256]{1,0:T(8,128)(2,1)S(1)} %collective-permute-done.5.a, bf16[512,256]{1,0:T(8,128)(2,1)S(1)} %collective-permute-done.3.got_c.c, ...), custom_call_target="tpu_custom_call" | custom-call | flops 3221225472 | bytes 16777216 | tf_op jit(solution)/shard_map/pallas_call | solution.py:509
  76.6 9.3 %all_to_all.22.parts_ref = f32[16,2,256]{2,1,0:T(2,128)S(1)} all-to-all(f32[16,2,256]{2,1,0:T(2,128)S(1)} %get-tuple-element.46), channel_id=1, replica_groups=mesh['parts_0'=4,'parts_1'=4,'parts_2'=8,'parts_3'=2] {'parts_0','parts_1'}, dimensions={0} | all-to-all | bytes 65536 | tf_op jit(solution)/shard_map/all_to_all | solution.py:375
  85.9 11.7 %all_to_all.23.stats_in_ref = f32[16,2,256]{2,1,0:T(2,128)S(1)} all-to-all(f32[16,2,256]{2,1,0:T(2,128)S(1)} %shard_map.99), channel_id=1, replica_groups=mesh['parts_0'=4,'parts_1'=4,'parts_2'=8,'parts_3'=2] {'parts_2','parts_3'}, dimensions={0} | all-to-all | bytes 65536 | tf_op jit(solution)/shard_map/all_to_all | solution.py:375
  97.6 1.4 %shard_map.100 = bf16[2048,256]{1,0:T(8,128)(2,1)} custom-call(bf16[2048,256]{1,0:T(8,128)(2,1)S(1)} %get-tuple-element.45.mixed_ref, f32[16,2,256]{2,1,0:T(2,128)S(1)} %all_to_all.23.stats_in_ref, f32[2,256]{1,0:T(2,128)S(1)} %copy-done.1, f32[2,256]{1,0:T(2,128)S(1)} %copy-done.2), custom_call_target="tpu_custom_call" | custom-call | tf_op jit(solution)/shard_map/pallas_call | solution.py:531
  (4 shorter events, 0.1 us)
Async XLA Ops:
  3.8 8.4 %collective-permute-start = (bf16[512,256]{1,0:T(8,128)(2,1)S(1)}, bf16[512,256]{1,0:T(8,128)(2,1)S(1)}, u32[]{:S(2)}, u32[]{:S(2)}) collective-permute-start(bf16[512,256]{1,0:T(8,128)(2,1)S(1)} %get-tuple-element.35), channel_id=1, source_target_pairs={{0,2},{2,0},{1,3},{3,1},{4,6},{6,4},{5,7},{7,5},{8,10},{10,8},{9,1... | collective-permute-start | bytes 786440 | tf_op jit(solution)/shard_map/ppermute | solution.py:25
  6.3 5.9 %collective-permute-start.1 = (bf16[512,256]{1,0:T(8,128)(2,1)S(1)}, bf16[512,256]{1,0:T(8,128)(2,1)S(1)}, u32[]{:S(2)}, u32[]{:S(2)}) collective-permute-start(bf16[512,256]{1,0:T(8,128)(2,1)S(1)} %get-tuple-element.36), channel_id=1, source_target_pairs={{2,4},{4,2},{3,5},{5,3},{6,8},{8,6},{7,9},{9,7},{10,12},{12,10},{1... | collective-permute-start | bytes 786440 | tf_op jit(solution)/shard_map/ppermute | solution.py:25
  9.8 5.4 %copy-start = (bf16[2,256,256]{2,1,0:T(8,128)(2,1)S(1)}, bf16[2,256,256]{2,1,0:T(8,128)(2,1)}, u32[]{:S(2)}) copy-start(bf16[2,256,256]{2,1,0:T(8,128)(2,1)} %weight_ref.3) | copy-start | bytes 786436
  12.2 2.9 %collective-permute-start.2 = (bf16[512,256]{1,0:T(8,128)(2,1)S(1)}, bf16[512,256]{1,0:T(8,128)(2,1)S(1)}, u32[]{:S(2)}, u32[]{:S(2)}) collective-permute-start(bf16[512,256]{1,0:T(8,128)(2,1)S(1)} %shard_map.94), channel_id=1, source_target_pairs={{0,1},{1,0},{2,3},{3,2},{4,5},{5,4},{6,7},{7,6},{8,9},{9,8},{10,11... | collective-permute-start | bytes 786440 | tf_op jit(solution)/shard_map/ppermute | solution.py:25
  15.2 54.7 %copy-start.1 = (f32[2,256]{1,0:T(2,128)S(1)}, f32[2,256]{1,0:T(2,128)}, u32[]{:S(2)}) copy-start(f32[2,256]{1,0:T(2,128)} %gain_ref.3) | copy-start | bytes 6148
  15.2 54.7 %copy-start.2 = (f32[2,256]{1,0:T(2,128)S(1)}, f32[2,256]{1,0:T(2,128)}, u32[]{:S(2)}) copy-start(f32[2,256]{1,0:T(2,128)} %shift_ref.3) | copy-start | bytes 6148
  19.8 11.2 %collective-permute-start.3 = (bf16[512,256]{1,0:T(8,128)(2,1)S(1)}, bf16[512,256]{1,0:T(8,128)(2,1)S(1)}, u32[]{:S(2)}, u32[]{:S(2)}) collective-permute-start(bf16[512,256]{1,0:T(8,128)(2,1)S(1)} %get-tuple-element.39), channel_id=1, source_target_pairs={{0,2},{2,0},{1,3},{3,1},{4,6},{6,4},{5,7},{7,5},{8,10},{10,8},{9,1... | collective-permute-start | bytes 786440 | tf_op jit(solution)/shard_map/ppermute | solution.py:25
  24.7 6.3 %collective-permute-start.4 = (bf16[512,256]{1,0:T(8,128)(2,1)S(1)}, bf16[512,256]{1,0:T(8,128)(2,1)S(1)}, u32[]{:S(2)}, u32[]{:S(2)}) collective-permute-start(bf16[512,256]{1,0:T(8,128)(2,1)S(1)} %get-tuple-element.40), channel_id=1, source_target_pairs={{2,4},{4,2},{3,5},{5,3},{6,8},{8,6},{7,9},{9,7},{10,12},{12,10},{1... | collective-permute-start | bytes 786440 | tf_op jit(solution)/shard_map/ppermute | solution.py:25
  31.1 38.8 %collective-permute-start.5 = (bf16[512,256]{1,0:T(8,128)(2,1)S(1)}, bf16[512,256]{1,0:T(8,128)(2,1)S(1)}, u32[]{:S(2)}, u32[]{:S(2)}) collective-permute-start(bf16[512,256]{1,0:T(8,128)(2,1)S(1)} %shard_map.96), channel_id=1, source_target_pairs={{0,1},{1,0},{2,3},{3,2},{4,5},{5,4},{6,7},{7,6},{8,9},{9,8},{10,11... | collective-permute-start | bytes 786440 | tf_op jit(solution)/shard_map/ppermute | solution.py:25
where the time goes:
time: 99.3 us; the launch traced here: 99 us
  blocking collectives  58.7 us (59%)
  Pallas kernels  21.1 us (21%)
  starting transfers between devices  11.6 us (12%)
  waiting for transfers between devices  6.81 us (7%)
    all_to_all x4, blocking collectives, from_peers(): return lax.all_to_all(stats, axes, 0, 0, tiled=True)  58.7 us
    ppermute x6, starting transfers between devices, swap(): return lax.ppermute(value, PARTS, pairs)  11.6 us
    ppermute x6, waiting for transfers between devices, swap(): return lax.ppermute(value, PARTS, pairs)  6.81 us
    pallas_call x1, Pallas kernels, shards(): pl.pallas_call(functools.partial(second_kernel, total), out_shape=[pltpu....  6.76 us
    pallas_call x1, Pallas kernels, shards(): pl.pallas_call(first_kernel, out_shape=[pltpu.VMEM(mixed.shape, bf16), pl...  4.61 us
    pallas_call x1, Pallas kernels, shards(): pl.pallas_call(functools.partial(gather_kernel, row_count, column_count,...  3.14 us
    pallas_call x1, Pallas kernels, shards(): pl.pallas_call(functools.partial(build_kernel, count, zeroed, loaded), ou...  2.81 us
    pallas_call x1, Pallas kernels, shards(): pl.pallas_call(own_kernel, out_shape=[pltpu.VMEM((height, channels), f32)...  2.35 us
  transfers between devices with their start and end apart: 6, of which 2 were waited for; matrix products, arithmetic and copies ran while one was open for 0% of the time, Pallas kernels for 5%

commit v1 on v0

--- a/solution.py
+++ b/solution.py
@@ -52,12 +52,6 @@
     piece_ref[pl.ds(at, count), :] = jnp.dot(
         one_hot_ref[pl.ds(first, count), :], rows_ref[...], preferred_element_type=jnp.float32
     ).astype(jnp.bfloat16)
-
-
-def pick_payloads(one_hot_ref, rows_ref, to_c, to_d):
-    size = to_c.shape[0]
-    pick_piece(one_hot_ref, rows_ref, to_c, 0, 0, size)
-    pick_piece(one_hot_ref, rows_ref, to_d, size, 0, size)
 
 
 def spread(row):
@@ -249,13 +243,13 @@
 
 
 def first_kernel(device_ref, recv_hot_ref, a, c, d, dense_ref, own_ref, weight_ref, send_hot_ref,
-                 z_ref, stats_ref, to_c, to_d, near_ref, dense_out,
-                 halo_ref, got_ref, moment_ref, left):
+                 z_ref, stats_out, to_c, to_d, near_ref, dense_out,
+                 halo_ref, got_ref, moment_ref, stats_ref, left):
     layer = 0
     count = a.shape[0] // 2
     written = own_ref.shape[0] // EDGE + 4 * count // EDGE - dense_out.shape[0]
     store = pltpu.make_async_copy(
-        dense_ref.at[pl.ds(written, dense_out.shape[0])], dense_out, left
+        dense_ref.at[pl.ds(written, dense_out.shape[0])], dense_out, left.at[0]
     )
     store.start()
     for n, piece in enumerate(received(a, c, d)):
@@ -283,9 +277,14 @@
         add_moments(z, moment_ref)
 
     put_moments(moment_ref, stats_ref)
-    pick_payloads(send_hot_ref, z_ref, to_c, to_d)
+    size = to_c.shape[0]
+    pick_piece(send_hot_ref, z_ref, to_c, 0, 0, size)
+    store_stats = pltpu.make_async_copy(stats_ref, stats_out, left.at[1])
+    store_stats.start()
+    pick_piece(send_hot_ref, z_ref, to_d, size, 0, size)
     put_near(device_ref, to_c, to_d, near_ref, 0)
     store.wait()
+    store_stats.wait()
 
 
 def scale_of(stats_ref, gain_ref, shift_ref, layer, vertex_total):
@@ -477,15 +476,16 @@
 
     z, stats, *sent, near, dense_b = pl.pallas_call(
         first_kernel,
-        out_shape=[pltpu.VMEM(mixed.shape, bf16), pltpu.VMEM(stats_type.shape, f32)]
+        out_shape=[pltpu.VMEM(mixed.shape, bf16), pltpu.HBM(stats_type.shape, f32)]
         + [payload] * 2 + [piece, pltpu.HBM((column_count - early, height, EDGE), bf16)],
         in_specs=[SMEM] + [VMEM] * 8,
-        out_specs=[VMEM] * 5 + [HBM],
+        out_specs=[VMEM, HBM] + [VMEM] * 3 + [HBM],
         scratch_shapes=[
             pltpu.VMEM((halo, channels), bf16),
             pltpu.VMEM((halo, channels), bf16),
             pltpu.VMEM((16, channels), f32),
-            pltpu.SemaphoreType.DMA,
+            pltpu.VMEM(stats_type.shape, f32),
+            pltpu.SemaphoreType.DMA((2,)),
         ],
         compiler_params=pltpu.CompilerParams(vmem_limit_bytes=12 * MIB),
         cost_estimate=pl.CostEstimate(

time: 99.3 us -> 100 us (level)
  no operation moved by 1% of the time
where the time goes in v1:
time: 100 us; the launch traced here: 99.8 us
  blocking collectives  58.9 us (59%)
  Pallas kernels  21.7 us (22%)
  starting transfers between devices  11.6 us (12%)
  waiting for transfers between devices  6.81 us (7%)
    all_to_all x4, blocking collectives, from_peers(): return lax.all_to_all(stats, axes, 0, 0, tiled=True)  58.9 us
    ppermute x6, starting transfers between devices, swap(): return lax.ppermute(value, PARTS, pairs)  11.6 us
    ppermute x6, waiting for transfers between devices, swap(): return lax.ppermute(value, PARTS, pairs)  6.81 us
    pallas_call x1, Pallas kernels, shards(): pl.pallas_call(functools.partial(second_kernel, total), out_shape=[pltpu....  6.76 us
    pallas_call x1, Pallas kernels, shards(): pl.pallas_call(first_kernel, out_shape=[pltpu.VMEM(mixed.shape, bf16), pl...  5.14 us
    pallas_call x1, Pallas kernels, shards(): pl.pallas_call(functools.partial(gather_kernel, row_count, column_count,...  3.14 us
    pallas_call x1, Pallas kernels, shards(): pl.pallas_call(functools.partial(build_kernel, count, zeroed, loaded), ou...  2.81 us
    pallas_call x1, Pallas kernels, shards(): pl.pallas_call(own_kernel, out_shape=[pltpu.VMEM((height, channels), f32)...  2.35 us
  transfers between devices with their start and end apart: 6, of which 2 were waited for; matrix products, arithmetic and copies ran while one was open for 0% of the time, Pallas kernels for 5%

profile of v1, /device:TPU:1, one launch (start us, length us, event | category | flops | bytes accessed | tf_op | source)
XLA Modules:
  0.0 99.8 jit_solution(12990657847973584657)
XLA Ops:
  0.7 3.1 %shard_map.91 = (bf16[512,256]{1,0:T(8,128)(2,1)S(1)}, bf16[512,256]{1,0:T(8,128)(2,1)S(1)}, bf16[256,256]{1,0:T(8,128)(2,1)S(1)}, bf16[1024,2048]{1,0:T(8,128)(...) custom-call(s32[1]{0:T(128)} %bitcast.device_ref, ...), custom_call_target="tpu_custom_call" | custom-call | flops 1073741824 | bytes 2097152 | tf_op jit(solution)/shard_map/pallas_call | solution.py:406
  3.8 2.5 %collective-permute-start = (bf16[512,256]{1,0:T(8,128)(2,1)S(1)}, bf16[512,256]{1,0:T(8,128)(2,1)S(1)}, u32[]{:S(2)}, u32[]{:S(2)}) collective-permute-start(bf16[512,256]{1,0:T(8,128)(2,1)S(1)} %get-tuple-element.35), channel_id=1, source_target_pairs={{0,2},{2,0},{1,3},{3,1},{4,6},{6,4},{5,7},{7,5},{8,10},{10,8},{9,1... | collective-permute-start | bytes 786440 | tf_op jit(solution)/shard_map/ppermute | solution.py:25
  6.3 0.7 collective-permute-start.1
  7.0 2.8 %shard_map.92 = (bf16[25,2048,128]{2,1,0:T(8,128)(2,1)S(1)}, bf16[256,128,128]{2,1,0:T(8,128)(2,1)S(1)}, bf16[1024,1024]{1,0:T(8,128)(2,1)S(1)}, s32[8,128]{1,0:T(8,128)S(1)}) custom-call(s32[1]{0:T(128)} %bitcast.device_ref, s32[4,256]{1,0:T(4,128)S(1)} %get-tuple-element.26.order_ref, ...), custom_call_target="tpu_custom_call", output_to_operand_aliasing={{0}: (5, {}), {1}: (6, {})} | custom-call | flops 4294967296 | bytes 25165824 | tf_op jit(solution)/shard_map/pallas_call | solution.py:431
  9.8 0.0 copy-start
  9.8 2.3 %shard_map.93 = (f32[2048,256]{1,0:T(8,128)S(1)}, bf16[8,2048,128]{2,1,0:T(8,128)(2,1)}) custom-call(bf16[25,2048,128]{2,1,0:T(8,128)(2,1)S(1)} %get-tuple-element.31.dense_ref, bf16[2048,256]{1,0:T(8,128)(2,1)S(1)} %get-tuple-element.32.rows_ref), custom_call_target="tpu_custom_call" | custom-call | flops 2147483648 | bytes 8388608 | tf_op jit(solution)/shard_map/pallas_call | solution.py:453
  12.2 0.0 collective-permute-done.got_c.c
  12.2 0.0 collective-permute-done.1.got_d.d
  12.2 1.8 %collective-permute-start.2 = (bf16[512,256]{1,0:T(8,128)(2,1)S(1)}, bf16[512,256]{1,0:T(8,128)(2,1)S(1)}, u32[]{:S(2)}, u32[]{:S(2)}) collective-permute-start(bf16[512,256]{1,0:T(8,128)(2,1)S(1)} %shard_map.94), channel_id=1, source_target_pairs={{0,1},{1,0},{2,3},{3,2},{4,5},{5,4},{6,7},{7,6},{8,9},{9,8},{10,11... | collective-permute-start | bytes 786440 | tf_op jit(solution)/shard_map/ppermute | solution.py:25
  14.0 1.2 %collective-permute-done.2.a = bf16[512,256]{1,0:T(8,128)(2,1)S(1)} collective-permute-done((bf16[512,256]{1,0:T(8,128)(2,1)S(1)}, bf16[512,256]{1,0:T(8,128)(2,1)S(1)}, u32[]{:S(2)}, u32[]{:S(2)}) %collective-permute-start.2) | collective-permute-done | bytes 262176 | tf_op jit(solution)/shard_map/ppermute | solution.py:25
  15.2 0.0 copy-done
  15.2 0.0 copy-start.1
  15.2 0.0 copy-start.2
  15.2 5.1 %shard_map.95 = (bf16[2048,256]{1,0:T(8,128)(2,1)S(1)}, f32[16,2,256]{2,1,0:T(2,128)}, bf16[512,256]{1,0:T(8,128)(2,1)S(1)}, bf16[512,256]{1,0:T(8,128)(2,1)S(1)...) custom-call(s32[1]{0:T(128)} %bitcast.device_ref, bf16[1024,1024]{1,0:T(8,128)(2,1)S(1)} %get-tuple-element.30.recv_hot_ref, ...), custom_call_target="tpu_custom_call" | custom-call | flops 1073741824 | bytes 16777216 | tf_op jit(solution)/shard_map/pallas_call | solution.py:477
  20.3 4.9 %collective-permute-start.3 = (bf16[512,256]{1,0:T(8,128)(2,1)S(1)}, bf16[512,256]{1,0:T(8,128)(2,1)S(1)}, u32[]{:S(2)}, u32[]{:S(2)}) collective-permute-start(bf16[512,256]{1,0:T(8,128)(2,1)S(1)} %get-tuple-element.39), channel_id=1, source_target_pairs={{0,2},{2,0},{1,3},{3,1},{4,6},{6,4},{5,7},{7,5},{8,10},{10,8},{9,1... | collective-permute-start | bytes 786440 | tf_op jit(solution)/shard_map/ppermute | solution.py:25
  25.3 0.7 collective-permute-start.4
  26.0 5.6 %collective-permute-done.3.got_c.c = bf16[512,256]{1,0:T(8,128)(2,1)S(1)} collective-permute-done((bf16[512,256]{1,0:T(8,128)(2,1)S(1)}, bf16[512,256]{1,0:T(8,128)(2,1)S(1)}, u32[]{:S(2)}, u32[]{:S(2)}) %collective-permute-start.3) | collective-permute-done | bytes 262176 | tf_op jit(solution)/shard_map/ppermute | solution.py:25
  31.6 0.0 collective-permute-done.4.got_d.d
  31.6 1.0 %collective-permute-start.5 = (bf16[512,256]{1,0:T(8,128)(2,1)S(1)}, bf16[512,256]{1,0:T(8,128)(2,1)S(1)}, u32[]{:S(2)}, u32[]{:S(2)}) collective-permute-start(bf16[512,256]{1,0:T(8,128)(2,1)S(1)} %shard_map.96), channel_id=1, source_target_pairs={{0,1},{1,0},{2,3},{3,2},{4,5},{5,4},{6,7},{7,6},{8,9},{9,8},{10,11... | collective-permute-start | bytes 786440 | tf_op jit(solution)/shard_map/ppermute | solution.py:25
  32.7 22.8 %all_to_all.20.parts_ref = f32[16,2,256]{2,1,0:T(2,128)S(1)} all-to-all(f32[16,2,256]{2,1,0:T(2,128)} %get-tuple-element.42), channel_id=1, replica_groups=mesh['parts_0'=4,'parts_1'=4,'parts_2'=8,'parts_3'=2] {'parts_0','parts_1'}, dimensions={0} | all-to-all | bytes 65536 | tf_op jit(solution)/shard_map/all_to_all | solution.py:374
  55.5 15.1 %all_to_all.21.stats_in_ref = f32[16,2,256]{2,1,0:T(2,128)S(1)} all-to-all(f32[16,2,256]{2,1,0:T(2,128)S(1)} %shard_map.97), channel_id=1, replica_groups=mesh['parts_0'=4,'parts_1'=4,'parts_2'=8,'parts_3'=2] {'parts_2','parts_3'}, dimensions={0} | all-to-all | bytes 65536 | tf_op jit(solution)/shard_map/all_to_all | solution.py:374
  70.6 0.0 collective-permute-done.5.a
  70.6 0.0 copy-done.1
  70.6 0.0 copy-done.2
  70.6 6.8 %shard_map.98 = (bf16[2048,256]{1,0:T(8,128)(2,1)S(1)}, f32[16,2,256]{2,1,0:T(2,128)S(1)}) custom-call(s32[1]{0:T(128)} %bitcast.device_ref, s32[8,128]{1,0:T(8,128)S(1)} %get-tuple-element.29.after_ref.index_ref, bf16[512,256]{1,0:T(8,128)(2,1)S(1)} %collective-permute-done.5.a, bf16[512,256]{1,0:T(8,128)(2,1)S(1)} %collective-permute-done.3.got_c.c, ...), custom_call_target="tpu_custom_call" | custom-call | flops 3221225472 | bytes 16777216 | tf_op jit(solution)/shard_map/pallas_call | solution.py:509
  77.4 9.3 %all_to_all.22.parts_ref = f32[16,2,256]{2,1,0:T(2,128)S(1)} all-to-all(f32[16,2,256]{2,1,0:T(2,128)S(1)} %get-tuple-element.46), channel_id=1, replica_groups=mesh['parts_0'=4,'parts_1'=4,'parts_2'=8,'parts_3'=2] {'parts_0','parts_1'}, dimensions={0} | all-to-all | bytes 65536 | tf_op jit(solution)/shard_map/all_to_all | solution.py:374
  86.7 11.7 %all_to_all.23.stats_in_ref = f32[16,2,256]{2,1,0:T(2,128)S(1)} all-to-all(f32[16,2,256]{2,1,0:T(2,128)S(1)} %shard_map.99), channel_id=1, replica_groups=mesh['parts_0'=4,'parts_1'=4,'parts_2'=8,'parts_3'=2] {'parts_2','parts_3'}, dimensions={0} | all-to-all | bytes 65536 | tf_op jit(solution)/shard_map/all_to_all | solution.py:374
  98.4 1.4 %shard_map.100 = bf16[2048,256]{1,0:T(8,128)(2,1)} custom-call(bf16[2048,256]{1,0:T(8,128)(2,1)S(1)} %get-tuple-element.45.mixed_ref, f32[16,2,256]{2,1,0:T(2,128)S(1)} %all_to_all.23.stats_in_ref, f32[2,256]{1,0:T(2,128)S(1)} %copy-done.1, f32[2,256]{1,0:T(2,128)S(1)} %copy-done.2), custom_call_target="tpu_custom_call" | custom-call | tf_op jit(solution)/shard_map/pallas_call | solution.py:531
  (4 shorter events, 0.1 us)
Async XLA Ops:
  3.8 8.4 %collective-permute-start = (bf16[512,256]{1,0:T(8,128)(2,1)S(1)}, bf16[512,256]{1,0:T(8,128)(2,1)S(1)}, u32[]{:S(2)}, u32[]{:S(2)}) collective-permute-start(bf16[512,256]{1,0:T(8,128)(2,1)S(1)} %get-tuple-element.35), channel_id=1, source_target_pairs={{0,2},{2,0},{1,3},{3,1},{4,6},{6,4},{5,7},{7,5},{8,10},{10,8},{9,1... | collective-permute-start | bytes 786440 | tf_op jit(solution)/shard_map/ppermute | solution.py:25
  6.3 5.9 %collective-permute-start.1 = (bf16[512,256]{1,0:T(8,128)(2,1)S(1)}, bf16[512,256]{1,0:T(8,128)(2,1)S(1)}, u32[]{:S(2)}, u32[]{:S(2)}) collective-permute-start(bf16[512,256]{1,0:T(8,128)(2,1)S(1)} %get-tuple-element.36), channel_id=1, source_target_pairs={{2,4},{4,2},{3,5},{5,3},{6,8},{8,6},{7,9},{9,7},{10,12},{12,10},{1... | collective-permute-start | bytes 786440 | tf_op jit(solution)/shard_map/ppermute | solution.py:25
  9.8 5.4 %copy-start = (bf16[2,256,256]{2,1,0:T(8,128)(2,1)S(1)}, bf16[2,256,256]{2,1,0:T(8,128)(2,1)}, u32[]{:S(2)}) copy-start(bf16[2,256,256]{2,1,0:T(8,128)(2,1)} %weight_ref.3) | copy-start | bytes 786436
  12.2 2.9 %collective-permute-start.2 = (bf16[512,256]{1,0:T(8,128)(2,1)S(1)}, bf16[512,256]{1,0:T(8,128)(2,1)S(1)}, u32[]{:S(2)}, u32[]{:S(2)}) collective-permute-start(bf16[512,256]{1,0:T(8,128)(2,1)S(1)} %shard_map.94), channel_id=1, source_target_pairs={{0,1},{1,0},{2,3},{3,2},{4,5},{5,4},{6,7},{7,6},{8,9},{9,8},{10,11... | collective-permute-start | bytes 786440 | tf_op jit(solution)/shard_map/ppermute | solution.py:25
  15.2 55.4 %copy-start.1 = (f32[2,256]{1,0:T(2,128)S(1)}, f32[2,256]{1,0:T(2,128)}, u32[]{:S(2)}) copy-start(f32[2,256]{1,0:T(2,128)} %gain_ref.3) | copy-start | bytes 6148
  15.2 55.4 %copy-start.2 = (f32[2,256]{1,0:T(2,128)S(1)}, f32[2,256]{1,0:T(2,128)}, u32[]{:S(2)}) copy-start(f32[2,256]{1,0:T(2,128)} %shift_ref.3) | copy-start | bytes 6148
  20.3 11.3 %collective-permute-start.3 = (bf16[512,256]{1,0:T(8,128)(2,1)S(1)}, bf16[512,256]{1,0:T(8,128)(2,1)S(1)}, u32[]{:S(2)}, u32[]{:S(2)}) collective-permute-start(bf16[512,256]{1,0:T(8,128)(2,1)S(1)} %get-tuple-element.39), channel_id=1, source_target_pairs={{0,2},{2,0},{1,3},{3,1},{4,6},{6,4},{5,7},{7,5},{8,10},{10,8},{9,1... | collective-permute-start | bytes 786440 | tf_op jit(solution)/shard_map/ppermute | solution.py:25
  25.3 6.3 %collective-permute-start.4 = (bf16[512,256]{1,0:T(8,128)(2,1)S(1)}, bf16[512,256]{1,0:T(8,128)(2,1)S(1)}, u32[]{:S(2)}, u32[]{:S(2)}) collective-permute-start(bf16[512,256]{1,0:T(8,128)(2,1)S(1)} %get-tuple-element.40), channel_id=1, source_target_pairs={{2,4},{4,2},{3,5},{5,3},{6,8},{8,6},{7,9},{9,7},{10,12},{12,10},{1... | collective-permute-start | bytes 786440 | tf_op jit(solution)/shard_map/ppermute | solution.py:25
  31.6 39.0 %collective-permute-start.5 = (bf16[512,256]{1,0:T(8,128)(2,1)S(1)}, bf16[512,256]{1,0:T(8,128)(2,1)S(1)}, u32[]{:S(2)}, u32[]{:S(2)}) collective-permute-start(bf16[512,256]{1,0:T(8,128)(2,1)S(1)} %shard_map.96), channel_id=1, source_target_pairs={{0,1},{1,0},{2,3},{3,2},{4,5},{5,4},{6,7},{7,6},{8,9},{9,8},{10,11... | collective-permute-start | bytes 786440 | tf_op jit(solution)/shard_map/ppermute | solution.py:25

commit v2 on v1

--- a/solution.py
+++ b/solution.py
@@ -202,21 +202,30 @@
     )
 
 
-def own_kernel(dense_ref, rows_ref, own_ref, dense_out, left):
-    store = pltpu.make_async_copy(
-        dense_ref.at[pl.ds(0, dense_out.shape[0])], dense_out, left
-    )
-    store.start()
-    height = own_ref.shape[0]
-    own_blocks = height // EDGE
+def put_own(dense_ref, rows_ref, own_ref, first, last):
+    own_blocks = own_ref.shape[0] // EDGE
     size = 512
-    for start in range(0, height, size):
+    for start in range(first, last, size):
         own_ref[pl.ds(start, size), :] = jnp.dot(
             adjacency_block(dense_ref, 0, own_blocks, start, size),
             rows_ref[...],
             preferred_element_type=jnp.float32,
         )
+
+
+def own_upper_kernel(dense_ref, rows_ref, own_ref, dense_out, left):
+    store = pltpu.make_async_copy(
+        dense_ref.at[pl.ds(0, dense_out.shape[0])], dense_out, left
+    )
+    store.start()
+    put_own(dense_ref, rows_ref, own_ref, 0, own_ref.shape[0] // 2)
     store.wait()
+
+
+def own_lower_kernel(after_ref, _own, dense_ref, rows_ref, own_ref):
+    del after_ref
+    height = own_ref.shape[0]
+    put_own(dense_ref, rows_ref, own_ref, height // 2, height)
 
 
 def add_moments(z, moment_ref):
@@ -400,7 +409,7 @@
     def in_hbm(value):
         return pltpu.with_memory_space_constraint(value, pltpu.HBM)
 
-    zeroed, loaded = column_count // 2, tile_values.shape[0] * 5 // 8
+    zeroed, loaded = column_count // 6, tile_values.shape[0] * 3 // 8
     dense_type = pltpu.VMEM((column_count + 1, height, EDGE), bf16)
     tiles_type = pltpu.VMEM(tile_values.shape, bf16)
     *sent, near, send_hot, order, rows, dense, tiles = pl.pallas_call(
@@ -449,9 +458,9 @@
     )(place, order, tile_count, in_hbm(recv_index), in_hbm(tile_values), on_chip(dense),
       on_chip(tiles))
 
-    early = column_count // 3
+    early = column_count // 4
     own, dense_a = pl.pallas_call(
-        own_kernel,
+        own_upper_kernel,
         out_shape=[
             pltpu.VMEM((height, channels), f32),
             pltpu.HBM((early, height, EDGE), bf16),
@@ -461,7 +470,7 @@
         scratch_shapes=[pltpu.SemaphoreType.DMA],
         compiler_params=pltpu.CompilerParams(vmem_limit_bytes=8 * MIB),
         cost_estimate=pl.CostEstimate(
-            flops=2 * height * height * channels, bytes_accessed=8 * MIB, transcendentals=0),
+            flops=height * height * channels, bytes_accessed=8 * MIB, transcendentals=0),
     )(on_chip(dense), on_chip(rows))
 
     relay_call = pl.pallas_call(
@@ -473,6 +482,17 @@
     )
     relay = relay_call(own, place, near, *got)
     got_core = core_swap(relay)
+
+    own = pl.pallas_call(
+        own_lower_kernel,
+        out_shape=pltpu.VMEM((height, channels), f32),
+        in_specs=[VMEM] * 4,
+        out_specs=VMEM,
+        input_output_aliases={1: 0},
+        compiler_params=pltpu.CompilerParams(vmem_limit_bytes=8 * MIB),
+        cost_estimate=pl.CostEstimate(
+            flops=height * height * channels, bytes_accessed=8 * MIB, transcendentals=0),
+    )(relay, on_chip(own), on_chip(dense), on_chip(rows))
 
     z, stats, *sent, near, dense_b = pl.pallas_call(
         first_kernel,

time: 100 us -> 100 us (level)
  waiting for transfers between devices: 6.81 us -> 5.78 us
    ppermute x6, waiting for transfers between devices: 6.81 us -> 5.78 us  [swap(): return lax.ppermute(value, PARTS, pairs)]
    pallas_call x1 -> x2, Pallas kernels: 2.35 us -> 2.92 us  [the longest x1 1.67 us: shards(): pl.pallas_call(own_upper_kernel, out_shape=[pltpu.VMEM((height, channels)...]
  transfers between devices with their start and end apart: 6 -> 6, of which waited for: 2 -> 1; matrix products, arithmetic and copies ran while one was open for 0% -> 0% of each run, Pallas kernels for 5% -> 6%
where the time goes in v2:
time: 100 us; the launch traced here: 99.7 us
  blocking collectives  58.9 us (59%)
  Pallas kernels  22.6 us (23%)
  starting transfers between devices  11.6 us (12%)
  waiting for transfers between devices  5.78 us (6%)
    all_to_all x4, blocking collectives, from_peers(): return lax.all_to_all(stats, axes, 0, 0, tiled=True)  58.9 us
    ppermute x6, starting transfers between devices, swap(): return lax.ppermute(value, PARTS, pairs)  11.6 us
    pallas_call x1, Pallas kernels, shards(): pl.pallas_call(functools.partial(second_kernel, total), out_shape=[pltpu....  6.75 us
    ppermute x6, waiting for transfers between devices, swap(): return lax.ppermute(value, PARTS, pairs)  5.78 us
    pallas_call x1, Pallas kernels, shards(): pl.pallas_call(first_kernel, out_shape=[pltpu.VMEM(mixed.shape, bf16), pl...  5.08 us
    pallas_call x1, Pallas kernels, shards(): pl.pallas_call(functools.partial(build_kernel, count, zeroed, loaded), ou...  3.41 us
    pallas_call x1, Pallas kernels, shards(): pl.pallas_call(functools.partial(gather_kernel, row_count, column_count,...  2.96 us
  transfers between devices with their start and end apart: 6, of which 1 were waited for; matrix products, arithmetic and copies ran while one was open for 0% of the time, Pallas kernels for 6%

profile of v2, /device:TPU:1, one launch (start us, length us, event | category | flops | bytes accessed | tf_op | source)
XLA Modules:
  0.0 99.7 jit_solution(1504368798482921935)
XLA Ops:
  0.7 3.0 %shard_map.91 = (bf16[512,256]{1,0:T(8,128)(2,1)S(1)}, bf16[512,256]{1,0:T(8,128)(2,1)S(1)}, bf16[256,256]{1,0:T(8,128)(2,1)S(1)}, bf16[1024,2048]{1,0:T(8,128)(...) custom-call(s32[1]{0:T(128)} %bitcast.device_ref, ...), custom_call_target="tpu_custom_call" | custom-call | flops 1073741824 | bytes 2097152 | tf_op jit(solution)/shard_map/pallas_call | solution.py:415
  3.6 2.5 %collective-permute-start = (bf16[512,256]{1,0:T(8,128)(2,1)S(1)}, bf16[512,256]{1,0:T(8,128)(2,1)S(1)}, u32[]{:S(2)}, u32[]{:S(2)}) collective-permute-start(bf16[512,256]{1,0:T(8,128)(2,1)S(1)} %get-tuple-element.35), channel_id=1, source_target_pairs={{0,2},{2,0},{1,3},{3,1},{4,6},{6,4},{5,7},{7,5},{8,10},{10,8},{9,1... | collective-permute-start | bytes 786440 | tf_op jit(solution)/shard_map/ppermute | solution.py:25
  6.2 0.7 collective-permute-start.1
  6.8 3.4 %shard_map.92 = (bf16[25,2048,128]{2,1,0:T(8,128)(2,1)S(1)}, bf16[256,128,128]{2,1,0:T(8,128)(2,1)S(1)}, bf16[1024,1024]{1,0:T(8,128)(2,1)S(1)}, s32[8,128]{1,0:T(8,128)S(1)}) custom-call(s32[1]{0:T(128)} %bitcast.device_ref, s32[4,256]{1,0:T(4,128)S(1)} %get-tuple-element.26.order_ref, ...), custom_call_target="tpu_custom_call", output_to_operand_aliasing={{0}: (5, {}), {1}: (6, {})} | custom-call | flops 4294967296 | bytes 25165824 | tf_op jit(solution)/shard_map/pallas_call | solution.py:440
  10.2 1.7 %shard_map.93 = (f32[2048,256]{1,0:T(8,128)S(1)}, bf16[6,2048,128]{2,1,0:T(8,128)(2,1)}) custom-call(bf16[25,2048,128]{2,1,0:T(8,128)(2,1)S(1)} %get-tuple-element.31.dense_ref, bf16[2048,256]{1,0:T(8,128)(2,1)S(1)} %get-tuple-element.32.rows_ref), custom_call_target="tpu_custom_call" | custom-call | flops 1073741824 | bytes 8388608 | tf_op jit(solution)/shard_map/pallas_call | solution.py:462
  11.9 0.0 collective-permute-done.got_c.c
  11.9 0.0 collective-permute-done.1.got_d.d
  12.0 0.0 copy-start
  12.0 1.8 %collective-permute-start.2 = (bf16[512,256]{1,0:T(8,128)(2,1)S(1)}, bf16[512,256]{1,0:T(8,128)(2,1)S(1)}, u32[]{:S(2)}, u32[]{:S(2)}) collective-permute-start(bf16[512,256]{1,0:T(8,128)(2,1)S(1)} %shard_map.94.after_ref), channel_id=1, source_target_pairs={{0,1},{1,0},{2,3},{3,2},{4,5},{5,4},{6,7},{7,6},{8,9},{9,8},{10,11... | collective-permute-start | bytes 786440 | tf_op jit(solution)/shard_map/ppermute | solution.py:25
  13.8 1.2 %shard_map.95.own_ref = f32[2048,256]{1,0:T(8,128)S(1)} custom-call(bf16[512,256]{1,0:T(8,128)(2,1)S(1)} %shard_map.94.after_ref, f32[2048,256]{1,0:T(8,128)S(1)} %get-tuple-element.33.after_ref._own, bf16[25,2048,128]{2,1,0:T(8,128)(2,1)S(1)} %get-tuple-element.31.dense_ref, ...), custom_call_target="tpu_custom_call", output_to_operand_aliasing={{}: (1, {})} | custom-call | flops 1073741824 | bytes 8388608 | tf_op jit(solution)/shard_map/pallas_call | solution.py:486
  15.0 0.0 collective-permute-done.2.a
  15.0 0.0 copy-done
  15.0 0.0 copy-start.1
  15.0 0.0 copy-start.2
  15.1 5.1 %shard_map.96 = (bf16[2048,256]{1,0:T(8,128)(2,1)S(1)}, f32[16,2,256]{2,1,0:T(2,128)}, bf16[512,256]{1,0:T(8,128)(2,1)S(1)}, bf16[512,256]{1,0:T(8,128)(2,1)S(1)...) custom-call(s32[1]{0:T(128)} %bitcast.device_ref, bf16[1024,1024]{1,0:T(8,128)(2,1)S(1)} %get-tuple-element.30.recv_hot_ref, ...), custom_call_target="tpu_custom_call" | custom-call | flops 1073741824 | bytes 16777216 | tf_op jit(solution)/shard_map/pallas_call | solution.py:497
  20.1 5.0 %collective-permute-start.3 = (bf16[512,256]{1,0:T(8,128)(2,1)S(1)}, bf16[512,256]{1,0:T(8,128)(2,1)S(1)}, u32[]{:S(2)}, u32[]{:S(2)}) collective-permute-start(bf16[512,256]{1,0:T(8,128)(2,1)S(1)} %get-tuple-element.39), channel_id=1, source_target_pairs={{0,2},{2,0},{1,3},{3,1},{4,6},{6,4},{5,7},{7,5},{8,10},{10,8},{9,1... | collective-permute-start | bytes 786440 | tf_op jit(solution)/shard_map/ppermute | solution.py:25
  25.2 0.7 collective-permute-start.4
  25.9 5.8 %collective-permute-done.3.got_c.c = bf16[512,256]{1,0:T(8,128)(2,1)S(1)} collective-permute-done((bf16[512,256]{1,0:T(8,128)(2,1)S(1)}, bf16[512,256]{1,0:T(8,128)(2,1)S(1)}, u32[]{:S(2)}, u32[]{:S(2)}) %collective-permute-start.3) | collective-permute-done | bytes 262176 | tf_op jit(solution)/shard_map/ppermute | solution.py:25
  31.6 0.0 collective-permute-done.4.got_d.d
  31.6 0.9 collective-permute-start.5
  32.6 22.8 %all_to_all.20.parts_ref = f32[16,2,256]{2,1,0:T(2,128)S(1)} all-to-all(f32[16,2,256]{2,1,0:T(2,128)} %get-tuple-element.42), channel_id=1, replica_groups=mesh['parts_0'=4,'parts_1'=4,'parts_2'=8,'parts_3'=2] {'parts_0','parts_1'}, dimensions={0} | all-to-all | bytes 65536 | tf_op jit(solution)/shard_map/all_to_all | solution.py:383
  55.4 15.1 %all_to_all.21.stats_in_ref = f32[16,2,256]{2,1,0:T(2,128)S(1)} all-to-all(f32[16,2,256]{2,1,0:T(2,128)S(1)} %shard_map.98), channel_id=1, replica_groups=mesh['parts_0'=4,'parts_1'=4,'parts_2'=8,'parts_3'=2] {'parts_2','parts_3'}, dimensions={0} | all-to-all | bytes 65536 | tf_op jit(solution)/shard_map/all_to_all | solution.py:383
  70.5 0.0 collective-permute-done.5.a
  70.5 0.0 copy-done.1
  70.5 0.0 copy-done.2
  70.5 6.8 %shard_map.99 = (bf16[2048,256]{1,0:T(8,128)(2,1)S(1)}, f32[16,2,256]{2,1,0:T(2,128)S(1)}) custom-call(s32[1]{0:T(128)} %bitcast.device_ref, s32[8,128]{1,0:T(8,128)S(1)} %get-tuple-element.29.after_ref.index_ref, bf16[512,256]{1,0:T(8,128)(2,1)S(1)} %collective-permute-done.5.a, bf16[512,256]{1,0:T(8,128)(2,1)S(1)} %collective-permute-done.3.got_c.c, ...), custom_call_target="tpu_custom_call" | custom-call | flops 3221225472 | bytes 16777216 | tf_op jit(solution)/shard_map/pallas_call | solution.py:529
  77.3 9.3 %all_to_all.22.parts_ref = f32[16,2,256]{2,1,0:T(2,128)S(1)} all-to-all(f32[16,2,256]{2,1,0:T(2,128)S(1)} %get-tuple-element.46), channel_id=1, replica_groups=mesh['parts_0'=4,'parts_1'=4,'parts_2'=8,'parts_3'=2] {'parts_0','parts_1'}, dimensions={0} | all-to-all | bytes 65536 | tf_op jit(solution)/shard_map/all_to_all | solution.py:383
  86.6 11.7 %all_to_all.23.stats_in_ref = f32[16,2,256]{2,1,0:T(2,128)S(1)} all-to-all(f32[16,2,256]{2,1,0:T(2,128)S(1)} %shard_map.100), channel_id=1, replica_groups=mesh['parts_0'=4,'parts_1'=4,'parts_2'=8,'parts_3'=2] {'parts_2','parts_3'}, dimensions={0} | all-to-all | bytes 65536 | tf_op jit(solution)/shard_map/all_to_all | solution.py:383
  98.3 1.4 %shard_map.101 = bf16[2048,256]{1,0:T(8,128)(2,1)} custom-call(bf16[2048,256]{1,0:T(8,128)(2,1)S(1)} %get-tuple-element.45.mixed_ref, f32[16,2,256]{2,1,0:T(2,128)S(1)} %all_to_all.23.stats_in_ref, f32[2,256]{1,0:T(2,128)S(1)} %copy-done.1, f32[2,256]{1,0:T(2,128)S(1)} %copy-done.2), custom_call_target="tpu_custom_call" | custom-call | tf_op jit(solution)/shard_map/pallas_call | solution.py:551
  (4 shorter events, 0.1 us)
Async XLA Ops:
  3.6 8.3 %collective-permute-start = (bf16[512,256]{1,0:T(8,128)(2,1)S(1)}, bf16[512,256]{1,0:T(8,128)(2,1)S(1)}, u32[]{:S(2)}, u32[]{:S(2)}) collective-permute-start(bf16[512,256]{1,0:T(8,128)(2,1)S(1)} %get-tuple-element.35), channel_id=1, source_target_pairs={{0,2},{2,0},{1,3},{3,1},{4,6},{6,4},{5,7},{7,5},{8,10},{10,8},{9,1... | collective-permute-start | bytes 786440 | tf_op jit(solution)/shard_map/ppermute | solution.py:25
  6.2 5.8 %collective-permute-start.1 = (bf16[512,256]{1,0:T(8,128)(2,1)S(1)}, bf16[512,256]{1,0:T(8,128)(2,1)S(1)}, u32[]{:S(2)}, u32[]{:S(2)}) collective-permute-start(bf16[512,256]{1,0:T(8,128)(2,1)S(1)} %get-tuple-element.36), channel_id=1, source_target_pairs={{2,4},{4,2},{3,5},{5,3},{6,8},{8,6},{7,9},{9,7},{10,12},{12,10},{1... | collective-permute-start | bytes 786440 | tf_op jit(solution)/shard_map/ppermute | solution.py:25
  12.0 3.0 %copy-start = (bf16[2,256,256]{2,1,0:T(8,128)(2,1)S(1)}, bf16[2,256,256]{2,1,0:T(8,128)(2,1)}, u32[]{:S(2)}) copy-start(bf16[2,256,256]{2,1,0:T(8,128)(2,1)} %weight_ref.3) | copy-start | bytes 786436
  12.0 3.0 %collective-permute-start.2 = (bf16[512,256]{1,0:T(8,128)(2,1)S(1)}, bf16[512,256]{1,0:T(8,128)(2,1)S(1)}, u32[]{:S(2)}, u32[]{:S(2)}) collective-permute-start(bf16[512,256]{1,0:T(8,128)(2,1)S(1)} %shard_map.94.after_ref), channel_id=1, source_target_pairs={{0,1},{1,0},{2,3},{3,2},{4,5},{5,4},{6,7},{7,6},{8,9},{9,8},{10,11... | collective-permute-start | bytes 786440 | tf_op jit(solution)/shard_map/ppermute | solution.py:25
  15.0 55.5 %copy-start.1 = (f32[2,256]{1,0:T(2,128)S(1)}, f32[2,256]{1,0:T(2,128)}, u32[]{:S(2)}) copy-start(f32[2,256]{1,0:T(2,128)} %gain_ref.3) | copy-start | bytes 6148
  15.0 55.5 %copy-start.2 = (f32[2,256]{1,0:T(2,128)S(1)}, f32[2,256]{1,0:T(2,128)}, u32[]{:S(2)}) copy-start(f32[2,256]{1,0:T(2,128)} %shift_ref.3) | copy-start | bytes 6148
  20.1 11.5 %collective-permute-start.3 = (bf16[512,256]{1,0:T(8,128)(2,1)S(1)}, bf16[512,256]{1,0:T(8,128)(2,1)S(1)}, u32[]{:S(2)}, u32[]{:S(2)}) collective-permute-start(bf16[512,256]{1,0:T(8,128)(2,1)S(1)} %get-tuple-element.39), channel_id=1, source_target_pairs={{0,2},{2,0},{1,3},{3,1},{4,6},{6,4},{5,7},{7,5},{8,10},{10,8},{9,1... | collective-permute-start | bytes 786440 | tf_op jit(solution)/shard_map/ppermute | solution.py:25
  25.2 6.4 %collective-permute-start.4 = (bf16[512,256]{1,0:T(8,128)(2,1)S(1)}, bf16[512,256]{1,0:T(8,128)(2,1)S(1)}, u32[]{:S(2)}, u32[]{:S(2)}) collective-permute-start(bf16[512,256]{1,0:T(8,128)(2,1)S(1)} %get-tuple-element.40), channel_id=1, source_target_pairs={{2,4},{4,2},{3,5},{5,3},{6,8},{8,6},{7,9},{9,7},{10,12},{12,10},{1... | collective-permute-start | bytes 786440 | tf_op jit(solution)/shard_map/ppermute | solution.py:25
  31.6 38.9 %collective-permute-start.5 = (bf16[512,256]{1,0:T(8,128)(2,1)S(1)}, bf16[512,256]{1,0:T(8,128)(2,1)S(1)}, u32[]{:S(2)}, u32[]{:S(2)}) collective-permute-start(bf16[512,256]{1,0:T(8,128)(2,1)S(1)} %shard_map.97), channel_id=1, source_target_pairs={{0,1},{1,0},{2,3},{3,2},{4,5},{5,4},{6,7},{7,6},{8,9},{9,8},{10,11... | collective-permute-start | bytes 786440 | tf_op jit(solution)/shard_map/ppermute | solution.py:25

commit v3 on v2

--- a/solution.py
+++ b/solution.py
@@ -369,9 +369,20 @@
     put_moments(moment_ref, stats_ref)
 
 
-def last_kernel(vertex_total, mixed_ref, stats_in_ref, gain_ref, shift_ref, out_ref):
+def last_kernel(vertex_total, mixed_ref, stats_in_ref, gain_ref, shift_ref, out_ref, held_ref, left):
     terms = scale_of(stats_in_ref, gain_ref, shift_ref, 1, vertex_total)
-    out_ref[...] = normal(mixed_ref[...], terms).astype(jnp.bfloat16)
+    parts = left.shape[0]
+    size = out_ref.shape[0] // parts
+    stores = []
+    for part in range(parts):
+        rows = pl.ds(part * size, size)
+        held_ref[rows, :] = normal(mixed_ref[rows, :], terms).astype(jnp.bfloat16)
+        stores.append(pltpu.make_async_copy(held_ref.at[rows], out_ref.at[rows], left.at[part]))
+        if part:
+            stores[part - 1].start()
+    stores[-1].start()
+    for store in stores:
+        store.wait()
 
 
 VMEM = pl.BlockSpec(memory_space=pltpu.VMEM)
@@ -552,7 +563,8 @@
         functools.partial(last_kernel, vertex_total),
         out_shape=mixed,
         in_specs=[VMEM] * 4,
-        out_specs=VMEM,
+        out_specs=HBM,
+        scratch_shapes=[pltpu.VMEM(mixed.shape, bf16), pltpu.SemaphoreType.DMA((8,))],
         compiler_params=pltpu.CompilerParams(vmem_limit_bytes=16 * MIB),
     )(on_chip(z), stats, norm_gain, norm_shift)
 

time: 100 us -> 99.8 us (level)
  no operation moved by 1% of the time
where the time goes in v3:
time: 99.8 us; the launch traced here: 99.5 us
  blocking collectives  58.9 us (59%)
  Pallas kernels  22.4 us (22%)
  starting transfers between devices  11.6 us (12%)
  waiting for transfers between devices  5.78 us (6%)
    all_to_all x4, blocking collectives, from_peers(): return lax.all_to_all(stats, axes, 0, 0, tiled=True)  58.9 us
    ppermute x6, starting transfers between devices, swap(): return lax.ppermute(value, PARTS, pairs)  11.6 us
    pallas_call x1, Pallas kernels, shards(): pl.pallas_call(functools.partial(second_kernel, total), out_shape=[pltpu....  6.75 us
    ppermute x6, waiting for transfers between devices, swap(): return lax.ppermute(value, PARTS, pairs)  5.78 us
    pallas_call x1, Pallas kernels, shards(): pl.pallas_call(first_kernel, out_shape=[pltpu.VMEM(mixed.shape, bf16), pl...  5.08 us
    pallas_call x1, Pallas kernels, shards(): pl.pallas_call(functools.partial(build_kernel, count, zeroed, loaded), ou...  3.41 us
    pallas_call x1, Pallas kernels, shards(): pl.pallas_call(functools.partial(gather_kernel, row_count, column_count,...  2.96 us
  transfers between devices with their start and end apart: 6, of which 1 were waited for; matrix products, arithmetic and copies ran while one was open for 0% of the time, Pallas kernels for 6%

profile of v3, /device:TPU:1, one launch (start us, length us, event | category | flops | bytes accessed | tf_op | source)
XLA Modules:
  0.0 99.5 jit_solution(2472441907314393198)
XLA Ops:
  0.7 3.0 %shard_map.91 = (bf16[512,256]{1,0:T(8,128)(2,1)S(1)}, bf16[512,256]{1,0:T(8,128)(2,1)S(1)}, bf16[256,256]{1,0:T(8,128)(2,1)S(1)}, bf16[1024,2048]{1,0:T(8,128)(...) custom-call(s32[1]{0:T(128)} %bitcast.device_ref, ...), custom_call_target="tpu_custom_call" | custom-call | flops 1073741824 | bytes 2097152 | tf_op jit(solution)/shard_map/pallas_call | solution.py:426
  3.6 2.5 %collective-permute-start = (bf16[512,256]{1,0:T(8,128)(2,1)S(1)}, bf16[512,256]{1,0:T(8,128)(2,1)S(1)}, u32[]{:S(2)}, u32[]{:S(2)}) collective-permute-start(bf16[512,256]{1,0:T(8,128)(2,1)S(1)} %get-tuple-element.35), channel_id=1, source_target_pairs={{0,2},{2,0},{1,3},{3,1},{4,6},{6,4},{5,7},{7,5},{8,10},{10,8},{9,1... | collective-permute-start | bytes 786440 | tf_op jit(solution)/shard_map/ppermute | solution.py:25
  6.2 0.7 collective-permute-start.1
  6.8 3.4 %shard_map.92 = (bf16[25,2048,128]{2,1,0:T(8,128)(2,1)S(1)}, bf16[256,128,128]{2,1,0:T(8,128)(2,1)S(1)}, bf16[1024,1024]{1,0:T(8,128)(2,1)S(1)}, s32[8,128]{1,0:T(8,128)S(1)}) custom-call(s32[1]{0:T(128)} %bitcast.device_ref, s32[4,256]{1,0:T(4,128)S(1)} %get-tuple-element.26.order_ref, ...), custom_call_target="tpu_custom_call", output_to_operand_aliasing={{0}: (5, {}), {1}: (6, {})} | custom-call | flops 4294967296 | bytes 25165824 | tf_op jit(solution)/shard_map/pallas_call | solution.py:451
  10.2 1.7 %shard_map.93 = (f32[2048,256]{1,0:T(8,128)S(1)}, bf16[6,2048,128]{2,1,0:T(8,128)(2,1)}) custom-call(bf16[25,2048,128]{2,1,0:T(8,128)(2,1)S(1)} %get-tuple-element.31.dense_ref, bf16[2048,256]{1,0:T(8,128)(2,1)S(1)} %get-tuple-element.32.rows_ref), custom_call_target="tpu_custom_call" | custom-call | flops 1073741824 | bytes 8388608 | tf_op jit(solution)/shard_map/pallas_call | solution.py:473
  11.9 0.0 collective-permute-done.got_c.c
  11.9 0.0 collective-permute-done.1.got_d.d
  12.0 0.0 copy-start
  12.0 1.8 %collective-permute-start.2 = (bf16[512,256]{1,0:T(8,128)(2,1)S(1)}, bf16[512,256]{1,0:T(8,128)(2,1)S(1)}, u32[]{:S(2)}, u32[]{:S(2)}) collective-permute-start(bf16[512,256]{1,0:T(8,128)(2,1)S(1)} %shard_map.94.after_ref), channel_id=1, source_target_pairs={{0,1},{1,0},{2,3},{3,2},{4,5},{5,4},{6,7},{7,6},{8,9},{9,8},{10,11... | collective-permute-start | bytes 786440 | tf_op jit(solution)/shard_map/ppermute | solution.py:25
  13.8 1.2 %shard_map.95.own_ref = f32[2048,256]{1,0:T(8,128)S(1)} custom-call(bf16[512,256]{1,0:T(8,128)(2,1)S(1)} %shard_map.94.after_ref, f32[2048,256]{1,0:T(8,128)S(1)} %get-tuple-element.33.after_ref._own, bf16[25,2048,128]{2,1,0:T(8,128)(2,1)S(1)} %get-tuple-element.31.dense_ref, ...), custom_call_target="tpu_custom_call", output_to_operand_aliasing={{}: (1, {})} | custom-call | flops 1073741824 | bytes 8388608 | tf_op jit(solution)/shard_map/pallas_call | solution.py:497
  15.0 0.0 collective-permute-done.2.a
  15.0 0.0 copy-done
  15.0 0.0 copy-start.1
  15.0 0.0 copy-start.2
  15.1 5.1 %shard_map.96 = (bf16[2048,256]{1,0:T(8,128)(2,1)S(1)}, f32[16,2,256]{2,1,0:T(2,128)}, bf16[512,256]{1,0:T(8,128)(2,1)S(1)}, bf16[512,256]{1,0:T(8,128)(2,1)S(1)...) custom-call(s32[1]{0:T(128)} %bitcast.device_ref, bf16[1024,1024]{1,0:T(8,128)(2,1)S(1)} %get-tuple-element.30.recv_hot_ref, ...), custom_call_target="tpu_custom_call" | custom-call | flops 1073741824 | bytes 16777216 | tf_op jit(solution)/shard_map/pallas_call | solution.py:508
  20.1 5.0 %collective-permute-start.3 = (bf16[512,256]{1,0:T(8,128)(2,1)S(1)}, bf16[512,256]{1,0:T(8,128)(2,1)S(1)}, u32[]{:S(2)}, u32[]{:S(2)}) collective-permute-start(bf16[512,256]{1,0:T(8,128)(2,1)S(1)} %get-tuple-element.39), channel_id=1, source_target_pairs={{0,2},{2,0},{1,3},{3,1},{4,6},{6,4},{5,7},{7,5},{8,10},{10,8},{9,1... | collective-permute-start | bytes 786440 | tf_op jit(solution)/shard_map/ppermute | solution.py:25
  25.2 0.7 collective-permute-start.4
  25.9 5.8 %collective-permute-done.3.got_c.c = bf16[512,256]{1,0:T(8,128)(2,1)S(1)} collective-permute-done((bf16[512,256]{1,0:T(8,128)(2,1)S(1)}, bf16[512,256]{1,0:T(8,128)(2,1)S(1)}, u32[]{:S(2)}, u32[]{:S(2)}) %collective-permute-start.3) | collective-permute-done | bytes 262176 | tf_op jit(solution)/shard_map/ppermute | solution.py:25
  31.6 0.0 collective-permute-done.4.got_d.d
  31.6 0.9 collective-permute-start.5
  32.6 22.8 %all_to_all.20.parts_ref = f32[16,2,256]{2,1,0:T(2,128)S(1)} all-to-all(f32[16,2,256]{2,1,0:T(2,128)} %get-tuple-element.42), channel_id=1, replica_groups=mesh['parts_0'=4,'parts_1'=4,'parts_2'=8,'parts_3'=2] {'parts_0','parts_1'}, dimensions={0} | all-to-all | bytes 65536 | tf_op jit(solution)/shard_map/all_to_all | solution.py:394
  55.4 15.1 %all_to_all.21.stats_in_ref = f32[16,2,256]{2,1,0:T(2,128)S(1)} all-to-all(f32[16,2,256]{2,1,0:T(2,128)S(1)} %shard_map.98), channel_id=1, replica_groups=mesh['parts_0'=4,'parts_1'=4,'parts_2'=8,'parts_3'=2] {'parts_2','parts_3'}, dimensions={0} | all-to-all | bytes 65536 | tf_op jit(solution)/shard_map/all_to_all | solution.py:394
  70.5 0.0 collective-permute-done.5.a
  70.5 0.0 copy-done.1
  70.5 0.0 copy-done.2
  70.5 6.8 %shard_map.99 = (bf16[2048,256]{1,0:T(8,128)(2,1)S(1)}, f32[16,2,256]{2,1,0:T(2,128)S(1)}) custom-call(s32[1]{0:T(128)} %bitcast.device_ref, s32[8,128]{1,0:T(8,128)S(1)} %get-tuple-element.29.after_ref.index_ref, bf16[512,256]{1,0:T(8,128)(2,1)S(1)} %collective-permute-done.5.a, bf16[512,256]{1,0:T(8,128)(2,1)S(1)} %collective-permute-done.3.got_c.c, ...), custom_call_target="tpu_custom_call" | custom-call | flops 3221225472 | bytes 16777216 | tf_op jit(solution)/shard_map/pallas_call | solution.py:540
  77.3 9.3 %all_to_all.22.parts_ref = f32[16,2,256]{2,1,0:T(2,128)S(1)} all-to-all(f32[16,2,256]{2,1,0:T(2,128)S(1)} %get-tuple-element.46), channel_id=1, replica_groups=mesh['parts_0'=4,'parts_1'=4,'parts_2'=8,'parts_3'=2] {'parts_0','parts_1'}, dimensions={0} | all-to-all | bytes 65536 | tf_op jit(solution)/shard_map/all_to_all | solution.py:394
  86.6 11.7 %all_to_all.23.stats_in_ref = f32[16,2,256]{2,1,0:T(2,128)S(1)} all-to-all(f32[16,2,256]{2,1,0:T(2,128)S(1)} %shard_map.100), channel_id=1, replica_groups=mesh['parts_0'=4,'parts_1'=4,'parts_2'=8,'parts_3'=2] {'parts_2','parts_3'}, dimensions={0} | all-to-all | bytes 65536 | tf_op jit(solution)/shard_map/all_to_all | solution.py:394
  98.3 1.2 %shard_map.101 = bf16[2048,256]{1,0:T(8,128)(2,1)} custom-call(bf16[2048,256]{1,0:T(8,128)(2,1)S(1)} %get-tuple-element.45.mixed_ref, f32[16,2,256]{2,1,0:T(2,128)S(1)} %all_to_all.23.stats_in_ref, f32[2,256]{1,0:T(2,128)S(1)} %copy-done.1, f32[2,256]{1,0:T(2,128)S(1)} %copy-done.2), custom_call_target="tpu_custom_call" | custom-call | tf_op jit(solution)/shard_map/pallas_call | solution.py:562
  (4 shorter events, 0.1 us)
Async XLA Ops:
  3.6 8.3 %collective-permute-start = (bf16[512,256]{1,0:T(8,128)(2,1)S(1)}, bf16[512,256]{1,0:T(8,128)(2,1)S(1)}, u32[]{:S(2)}, u32[]{:S(2)}) collective-permute-start(bf16[512,256]{1,0:T(8,128)(2,1)S(1)} %get-tuple-element.35), channel_id=1, source_target_pairs={{0,2},{2,0},{1,3},{3,1},{4,6},{6,4},{5,7},{7,5},{8,10},{10,8},{9,1... | collective-permute-start | bytes 786440 | tf_op jit(solution)/shard_map/ppermute | solution.py:25
  6.2 5.8 %collective-permute-start.1 = (bf16[512,256]{1,0:T(8,128)(2,1)S(1)}, bf16[512,256]{1,0:T(8,128)(2,1)S(1)}, u32[]{:S(2)}, u32[]{:S(2)}) collective-permute-start(bf16[512,256]{1,0:T(8,128)(2,1)S(1)} %get-tuple-element.36), channel_id=1, source_target_pairs={{2,4},{4,2},{3,5},{5,3},{6,8},{8,6},{7,9},{9,7},{10,12},{12,10},{1... | collective-permute-start | bytes 786440 | tf_op jit(solution)/shard_map/ppermute | solution.py:25
  12.0 3.0 %copy-start = (bf16[2,256,256]{2,1,0:T(8,128)(2,1)S(1)}, bf16[2,256,256]{2,1,0:T(8,128)(2,1)}, u32[]{:S(2)}) copy-start(bf16[2,256,256]{2,1,0:T(8,128)(2,1)} %weight_ref.3) | copy-start | bytes 786436
  12.0 3.0 %collective-permute-start.2 = (bf16[512,256]{1,0:T(8,128)(2,1)S(1)}, bf16[512,256]{1,0:T(8,128)(2,1)S(1)}, u32[]{:S(2)}, u32[]{:S(2)}) collective-permute-start(bf16[512,256]{1,0:T(8,128)(2,1)S(1)} %shard_map.94.after_ref), channel_id=1, source_target_pairs={{0,1},{1,0},{2,3},{3,2},{4,5},{5,4},{6,7},{7,6},{8,9},{9,8},{10,11... | collective-permute-start | bytes 786440 | tf_op jit(solution)/shard_map/ppermute | solution.py:25
  15.0 55.5 %copy-start.1 = (f32[2,256]{1,0:T(2,128)S(1)}, f32[2,256]{1,0:T(2,128)}, u32[]{:S(2)}) copy-start(f32[2,256]{1,0:T(2,128)} %gain_ref.3) | copy-start | bytes 6148
  15.0 55.5 %copy-start.2 = (f32[2,256]{1,0:T(2,128)S(1)}, f32[2,256]{1,0:T(2,128)}, u32[]{:S(2)}) copy-start(f32[2,256]{1,0:T(2,128)} %shift_ref.3) | copy-start | bytes 6148
  20.1 11.5 %collective-permute-start.3 = (bf16[512,256]{1,0:T(8,128)(2,1)S(1)}, bf16[512,256]{1,0:T(8,128)(2,1)S(1)}, u32[]{:S(2)}, u32[]{:S(2)}) collective-permute-start(bf16[512,256]{1,0:T(8,128)(2,1)S(1)} %get-tuple-element.39), channel_id=1, source_target_pairs={{0,2},{2,0},{1,3},{3,1},{4,6},{6,4},{5,7},{7,5},{8,10},{10,8},{9,1... | collective-permute-start | bytes 786440 | tf_op jit(solution)/shard_map/ppermute | solution.py:25
  25.2 6.4 %collective-permute-start.4 = (bf16[512,256]{1,0:T(8,128)(2,1)S(1)}, bf16[512,256]{1,0:T(8,128)(2,1)S(1)}, u32[]{:S(2)}, u32[]{:S(2)}) collective-permute-start(bf16[512,256]{1,0:T(8,128)(2,1)S(1)} %get-tuple-element.40), channel_id=1, source_target_pairs={{2,4},{4,2},{3,5},{5,3},{6,8},{8,6},{7,9},{9,7},{10,12},{12,10},{1... | collective-permute-start | bytes 786440 | tf_op jit(solution)/shard_map/ppermute | solution.py:25
  31.6 38.9 %collective-permute-start.5 = (bf16[512,256]{1,0:T(8,128)(2,1)S(1)}, bf16[512,256]{1,0:T(8,128)(2,1)S(1)}, u32[]{:S(2)}, u32[]{:S(2)}) collective-permute-start(bf16[512,256]{1,0:T(8,128)(2,1)S(1)} %shard_map.97), channel_id=1, source_target_pairs={{0,1},{1,0},{2,3},{3,2},{4,5},{5,4},{6,7},{7,6},{8,9},{9,8},{10,11... | collective-permute-start | bytes 786440 | tf_op jit(solution)/shard_map/ppermute | solution.py:25
